TPU v7x, 32 devices: a whole 2x2x4 slice. The times are simulated.
32 devices in a mesh: sub: 2 (over y), row: 4 (over x, core), col: 4 (over z).
Axes of the slice: x: 2, y: 2, z: 4, core: 2. Of those that a mesh axis runs over, the one named last changes fastest.
Arguments:
- factor_window: bfloat16 [2, 8192, 1024], P('sub', ('row', 'col'))
- right_sides: bfloat16 [2, 8192, 2048], P('sub', 'row', 'col'), may hold values from -1.1953125 to 1.1953125
- first_block: int32 [2, 8], P('sub'), may hold values from 0 to 4
- tile_map: int32 [2, 8], P('sub'), may hold values from 0 to 15, as said below
- interface_block: float32 [4096, 4096], P(('sub', 'row'), 'col'), may hold values from -6 to 6
Outputs:
- updated_sides: bfloat16 [2, 8192, 2048], P('sub', 'row', 'col')
- schur_global: float32 [4096, 4096], P(('sub', 'row'), 'col')
Inputs may be any that keep to these rules, and one draw needn't show every extreme that they name: `tile_map`: the 8 entries of a subdomain are different global tiles.
All inputs are finite; a program needn't handle non-finite values.
Results may differ from a plain program's by a relative error of at most 0.0075.
Values may be sent and summed in bfloat16 or wider, within the bound.
A program may use at most 64 MiB of HBM per device.

v0:
```python
import jax
import jax.numpy as jnp
from jax import lax
from jax.sharding import PartitionSpec as P

PANEL = 256
BLOCK = 256
STEPS = 4
GTILES = 16


def spread_2(value, axis, source):
    kept = jnp.where(lax.axis_index(axis) == source, value, 0).astype(value.dtype)
    return lax.psum(kept, axis)


def spread_tiles(columns, tile_map, block_count):
    onehot = (tile_map[0][:, None] == jnp.arange(GTILES, dtype=jnp.int32)[None, :]).astype(
        jnp.bfloat16
    )
    height = columns.shape[0]
    spread = jnp.einsum(
        "qbj,bg->qgj",
        columns.reshape(height, block_count, BLOCK),
        onehot,
        preferred_element_type=jnp.float32,
    )
    return spread.reshape(height, GTILES * BLOCK).astype(jnp.bfloat16)


def local(factor_window, right_sides, first_block, tile_map, interface_block):
    row_count = lax.axis_size("row")
    row_pos = lax.axis_index("row")
    col_pos = lax.axis_index("col")
    local_factor = factor_window[0]
    local_sides = right_sides[0]
    block_rows = local_sides.shape[0]
    block_cols = local_sides.shape[1]
    block_count = first_block.shape[1]
    row_global = row_pos * block_rows + jnp.arange(block_rows, dtype=jnp.int32)
    col_global = col_pos * block_cols + jnp.arange(block_cols, dtype=jnp.int32)
    col_block = col_global // BLOCK
    block_ids = jnp.arange(block_count, dtype=jnp.int32)
    first_col = jnp.sum(
        jnp.where(col_block[:, None] == block_ids[None, :], first_block[0][None, :], 0), axis=1
    )
    live = (row_global // PANEL)[:, None] >= first_col[None, :]
    current = jnp.where(live, local_sides.astype(jnp.float32), jnp.float32(0.0))
    is_root = row_pos == 0
    factor_rows = lax.all_gather(local_factor, "col", axis=0, tiled=True)
    pieces = []
    for panel in range(STEPS):
        offset = panel * PANEL
        panel_cols = factor_rows[:, offset : offset + PANEL]
        diag_block = panel_cols[offset : offset + PANEL].astype(jnp.float32)
        diag_block = jnp.where(is_root, diag_block, jnp.eye(PANEL, dtype=jnp.float32))
        solved = jax.scipy.linalg.solve_triangular(
            diag_block, current[offset : offset + PANEL], lower=True
        ).astype(jnp.bfloat16)
        solved = spread_2(solved, "row", 0)
        update = jnp.dot(panel_cols, solved, preferred_element_type=jnp.float32)
        current = jnp.where((row_global >= offset + PANEL)[:, None], current - update, current)
        placed = jnp.where(is_root, solved.astype(jnp.float32), current[offset : offset + PANEL])
        current = current.at[offset : offset + PANEL].set(placed)
        pieces.append(solved)
    updated_sides = current.astype(jnp.bfloat16)[None]
    stacked = jnp.concatenate(pieces, axis=0)
    out_cols = interface_block.shape[1]
    share = stacked.shape[0] // row_count
    my_share = lax.dynamic_slice_in_dim(stacked, row_pos * share, share, 0)
    all_columns = lax.all_gather(my_share, "col", axis=1, tiled=True)
    spread = spread_tiles(all_columns, tile_map, block_count)
    my_columns = lax.dynamic_slice_in_dim(spread, col_pos * out_cols, out_cols, 1)
    summed = lax.psum_scatter(
        lax.dot_general(
            spread, my_columns, (((0,), (0,)), ((), ())), preferred_element_type=jnp.float32
        ).astype(jnp.bfloat16),
        ("sub", "row"),
        scatter_dimension=0,
        tiled=True,
    ).astype(jnp.float32)
    schur_global = interface_block - summed
    return (updated_sides, schur_global)


def solution(mesh):
    return jax.shard_map(
        local,
        mesh=mesh,
        in_specs=(
            P("sub", ("row", "col"), None),
            P("sub", "row", "col"),
            P("sub", None),
            P("sub", None),
            P(("sub", "row"), "col"),
        ),
        out_specs=(P("sub", "row", "col"), P(("sub", "row"), "col")),
        check_vma=False,
    )
```

profile of v0, /device:TPU:0, one launch (start us, length us, event | category | flops | bytes accessed | tf_op | source)
XLA Modules:
  0.0 394.8 jit_solution(10873900418680429173)
XLA Ops:
  8.8 3.5 convert_select_fusion
  12.3 80.8 %all-gather.6.cloned.1.call-done = bf16[1,2048,1024]{2,1,0:T(8,128)(2,1)} async-done(((bf16[1,512,1024]{2,1,0:T(8,128)(2,1)}), bf16[1,2048,1024]{2,1,0:T(8,128)(2,1)}) %all-gather.6.cloned.1.call-update) | async-done | bytes 4194320 | tf_op jit(solution)/shard_map/all_gather | solution.py:50
  94.3 3.8 while.12
  98.1 19.7 %custom-call.6 = f32[2,128,128]{1,2,0:T(8,128)S(1)} custom-call(f32[2,128,128]{2,1,0:T(8,128)S(1)} %get-tuple-element.77), custom_call_target="InvertDiagBlocksLowerTriangular" | custom-call | tf_op jit(solution)/shard_map/jit(_solve_triangular)/triangular_solve | solution.py:57
  121.7 4.0 %while.13 = (s32[]{:T(128)}, f32[256,256]{1,0:T(8,128)S(1)}, s32[2,2]{1,0:T(2,128)S(1)}, f32[2,128,128]{2,1,0:T(8,128)S(1)}, s32[]{:T(128)}) while((s32[]{:T(128)}, f32[256,256]{1,0:T(8,128)S(1)}, s32[2,2]{1,0:T(2,128)S(1)}, f32[2,128,128]{2,1,0:T(8,128)S(1)}, s32[]{:T(128)}) %tuple.113), condition=%wide.while_cond.4.clone, body=%wide.while_body.4.clone.sunk | while | flops 2 | bytes 131181 | solution.py:57
  125.8 19.7 %custom-call.7 = f32[2,128,128]{1,2,0:T(8,128)S(1)} custom-call(f32[2,128,128]{2,1,0:T(8,128)S(1)} %get-tuple-element.78), custom_call_target="InvertDiagBlocksLowerTriangular" | custom-call | tf_op jit(solution)/shard_map/jit(_solve_triangular)/triangular_solve | solution.py:57
  145.5 7.4 %all-reduce.5.cloned.1.call-done = bf16[256,512]{1,0:T(8,128)(2,1)} async-done(((bf16[256,512]{1,0:T(8,128)(2,1)}), bf16[256,512]{1,0:T(8,128)(2,1)}) %all-reduce.5.cloned.1.call-update) | async-done | bytes 262160 | tf_op jit(solution)/shard_map/psum | solution.py:14
  152.9 3.4 subtract_select_fusion.3
  160.2 4.0 %while.14 = (s32[]{:T(128)}, f32[256,256]{1,0:T(8,128)S(1)}, s32[2,2]{1,0:T(2,128)S(1)}, f32[2,128,128]{2,1,0:T(8,128)S(1)}, s32[]{:T(128)}) while((s32[]{:T(128)}, f32[256,256]{1,0:T(8,128)S(1)}, s32[2,2]{1,0:T(2,128)S(1)}, f32[2,128,128]{2,1,0:T(8,128)S(1)}, s32[]{:T(128)}) %tuple.114), condition=%wide.while_cond.4.clone.1, body=%wide.while_body.4.clone.1.sunk | while | flops 2 | bytes 131181 | solution.py:57
  164.2 19.7 %custom-call.8 = f32[2,128,128]{1,2,0:T(8,128)S(1)} custom-call(f32[2,128,128]{2,1,0:T(8,128)S(1)} %get-tuple-element.79), custom_call_target="InvertDiagBlocksLowerTriangular" | custom-call | tf_op jit(solution)/shard_map/jit(_solve_triangular)/triangular_solve | solution.py:57
  183.9 8.8 %all-reduce.7.cloned.1.call-done = bf16[256,512]{1,0:T(8,128)(2,1)} async-done(((bf16[256,512]{1,0:T(8,128)(2,1)}), bf16[256,512]{1,0:T(8,128)(2,1)}) %all-reduce.7.cloned.1.call-update) | async-done | bytes 262160 | tf_op jit(solution)/shard_map/psum | solution.py:14
  192.7 3.4 subtract_select_fusion.2
  196.7 1.6 copy-done.1
  199.9 3.8 while.15
  203.7 19.7 %custom-call.9 = f32[2,128,128]{1,2,0:T(8,128)S(1)} custom-call(f32[2,128,128]{2,1,0:T(8,128)S(1)} %get-tuple-element.80), custom_call_target="InvertDiagBlocksLowerTriangular" | custom-call | tf_op jit(solution)/shard_map/jit(_solve_triangular)/triangular_solve | solution.py:57
  223.4 9.2 %all-reduce.9.cloned.1.call-done = bf16[256,512]{1,0:T(8,128)(2,1)} async-done(((bf16[256,512]{1,0:T(8,128)(2,1)}), bf16[256,512]{1,0:T(8,128)(2,1)}) %all-reduce.9.cloned.1.call-update) | async-done | bytes 262160 | tf_op jit(solution)/shard_map/psum | solution.py:14
  232.5 3.4 subtract_select_fusion.1
  239.7 32.3 %all-reduce.11.cloned.1.call-done = bf16[256,512]{1,0:T(8,128)(2,1)} async-done(((bf16[256,512]{1,0:T(8,128)(2,1)}), bf16[256,512]{1,0:T(8,128)(2,1)}) %all-reduce.11.cloned.1.call-update) | async-done | bytes 262160 | tf_op jit(solution)/shard_map/psum | solution.py:14
  272.0 3.4 subtract_select_fusion
  275.4 1.6 fusion.19
  277.2 27.9 %all-gather.4.cloned.1.call-done = bf16[256,2048]{1,0:T(8,128)(2,1)} async-done(((bf16[256,512]{1,0:T(8,128)(2,1)}), bf16[256,2048]{1,0:T(8,128)(2,1)}) %all-gather.4.cloned.1.call-update) | async-done | bytes 1048592 | tf_op jit(solution)/shard_map/all_gather | solution.py:71
  308.4 5.6 %convolution_convert_fusion = bf16[4096,1024]{1,0:T(8,128)(2,1)} fusion(bf16[256,4096]{1,0:T(8,128)(2,1)S(1)} %bitcast.105, s32[]{:T(128)S(6)} %select_n.126), kind=kOutput, calls=%fused_computation.8 | convolution fusion | flops 2151677952 | bytes 11010052 | tf_op jit(solution)/shard_map/dot_general | solution.py:75
  314.1 71.0 %reduce-scatter.2.cloned.1.call-done = bf16[512,1024]{1,0:T(8,128)(2,1)} async-done(((bf16[4096,1024]{1,0:T(8,128)(2,1)}), bf16[512,1024]{1,0:T(8,128)(2,1)}) %reduce-scatter.2.cloned.1.call-update) | async-done | bytes 1048592 | tf_op jit(solution)/shard_map/reduce_scatter | solution.py:74
  385.1 2.8 convert_subtract_fusion
  (95 shorter events, 35.5 us)
Async XLA Ops:
  7.2 85.9 %all-gather.6.cloned.1.call-start = ((), (), s32[]{:S(2)}) async-start(), calls=%async_computation.7 | async-start | bytes 5242880 | tf_op jit(solution)/shard_map/all_gather | solution.py:50
  7.9 145.0 %all-reduce.5.cloned.1.call-start = ((), (), s32[]{:S(2)}) async-start(), calls=%async_computation.1 | async-start | bytes 524288 | tf_op jit(solution)/shard_map/psum | solution.py:14
  12.3 140.6 %copy-start.6 = (bf16[1,2048,512]{2,1,0:T(8,128)(2,1)S(1)}, bf16[1,2048,512]{2,1,0:T(8,128)(2,1)}, u32[]{:S(2)}) copy-start(bf16[1,2048,512]{2,1,0:T(8,128)(2,1)} %param.16) | copy-start | bytes 6291460
  121.7 71.0 %all-reduce.7.cloned.1.call-start = ((), (), s32[]{:S(2)}) async-start(), calls=%async_computation.2 | async-start | bytes 524288 | tf_op jit(solution)/shard_map/psum | solution.py:14
  152.9 3.4 copy-start.8
  156.4 2.0 copy-start.2
  160.0 72.6 %all-reduce.9.cloned.1.call-start = ((), (), s32[]{:S(2)}) async-start(), calls=%async_computation.3 | async-start | bytes 524288 | tf_op jit(solution)/shard_map/psum | solution.py:14
  192.7 3.4 copy-start.4
  196.2 2.0 copy-start.1
  199.8 72.2 %all-reduce.11.cloned.1.call-start = ((), (), s32[]{:S(2)}) async-start(), calls=%async_computation.4 | async-start | bytes 524288 | tf_op jit(solution)/shard_map/psum | solution.py:14
  232.5 3.4 copy-start.5
  236.0 2.0 copy-start
  239.6 65.5 %all-gather.4.cloned.1.call-start = ((), (), s32[]{:S(2)}) async-start(), calls=%async_computation.5 | async-start | bytes 1310720 | tf_op jit(solution)/shard_map/all_gather | solution.py:71
  239.7 67.0 %copy-start.10 = (s32[1,8]{1,0:T(1,128)S(1)}, s32[1,8]{1,0:T(1,128)}, u32[]{:S(2)}) copy-start(s32[1,8]{1,0:T(1,128)} %param.18) | copy-start | bytes 100
  272.0 3.4 copy-start.9
  276.9 31.5 %copy-start.3 = (bf16[2048,512]{1,0:T(8,128)(2,1)}, bf16[2048,512]{1,0:T(8,128)(2,1)S(1)}, u32[]{:S(2)}) copy-start(bf16[2048,512]{1,0:T(8,128)(2,1)S(1)} %get-tuple-element.126) | copy-start | bytes 6291460
  277.0 108.2 %reduce-scatter.2.cloned.1.call-start = ((), (), s32[]{:S(2)}) async-start(), calls=%async_computation.6 | async-start | bytes 9437184 | tf_op jit(solution)/shard_map/reduce_scatter | solution.py:74
  314.1 71.1 %copy-start.7 = (f32[512,1024]{1,0:T(8,128)S(1)}, f32[512,1024]{1,0:T(8,128)}, u32[]{:S(2)}) copy-start(f32[512,1024]{1,0:T(8,128)} %param.19) | copy-start | bytes 6291460
Sparse Core Ops, SparseCore 0:
  9.5 83.4 all-gather.5
  121.8 31.0 all-reduce.4
  160.1 32.5 all-reduce.6
  199.9 32.5 all-reduce.8
  239.7 32.2 all-reduce.10
  277.1 27.9 all-gather.3
  314.2 70.8 reduce-scatter.1
where the time goes:
time: 395 us
  waiting for transfers between devices  238 us (60%)
  other arithmetic  92 us (23%)
  matrix products  26.7 us (7%)
  local copies, waits for them, and re-layouts  22.7 us (6%)
  between operations  14.5 us (4%)
    all_gather x1, waiting for transfers between devices, local(): factor_rows = lax.all_gather(local_factor, 'col', axis=0, tiled=True)  80.8 us
    another operation x6, other arithmetic, local(): jax.scipy.linalg.solve_triangular(diag_block, current[offset:offset + PAN...  79.9 us
    reduce_scatter x1, waiting for transfers between devices, local(): lax.psum_scatter(lax.dot_general(spread, my_columns, (((0,), (0,)), ((),...  71 us
    psum x4, waiting for transfers between devices, spread_2(): return lax.psum(kept, axis)  57.7 us
    all_gather x1, waiting for transfers between devices, local(): all_columns = lax.all_gather(my_share, 'col', axis=1, tiled=True)  27.9 us
    another operation x29, local copies, waits for them, and re-layouts, local(): jax.scipy.linalg.solve_triangular(diag_block, current[offset:offset + PAN...  15.5 us
    dot_general x4, matrix products, local(): update = jnp.dot(panel_cols, solved, preferred_element_type=jnp.float32)  13.4 us
  transfers between devices with their start and end apart: 7, of which 7 were waited for; matrix products, arithmetic and copies ran while one was open for 19% of the time, Pallas kernels for 0%

commit v1 on v0

--- a/solution.py
+++ b/solution.py
@@ -1,3 +1,4 @@
+import functools
 import jax
 import jax.numpy as jnp
 from jax import lax
@@ -7,6 +8,26 @@
 BLOCK = 256
 STEPS = 4
 GTILES = 16
+
+
+def meet_fields(frame_in, across):
+    samples = [frame_in]
+    dev_i = 0
+    how_many = lax.psum(1, axis_name=across)
+    while dev_i < how_many - 1:
+        next_value = lax.ppermute(
+            samples[-1],
+            axis_name=across,
+            perm=[(no, (no + 1) % how_many) for no in range(how_many)],
+        )
+        samples.append(next_value)
+        dev_i += 1
+    top = jnp.concatenate(samples[::-1], 1)
+    arr_next = lax.axis_index(across)
+    return jnp.roll(top, (arr_next + 1) * frame_in.shape[1], 1)
+
+
+widths_handle = functools.partial(meet_fields, across="col")
 
 
 def spread_2(value, axis, source):
@@ -68,7 +89,7 @@
     out_cols = interface_block.shape[1]
     share = stacked.shape[0] // row_count
     my_share = lax.dynamic_slice_in_dim(stacked, row_pos * share, share, 0)
-    all_columns = lax.all_gather(my_share, "col", axis=1, tiled=True)
+    all_columns = widths_handle(my_share)
     spread = spread_tiles(all_columns, tile_map, block_count)
     my_columns = lax.dynamic_slice_in_dim(spread, col_pos * out_cols, out_cols, 1)
     summed = lax.psum_scatter(

time: 395 us -> 389 us (0.985)
  waiting for transfers between devices: 238 us -> 232 us
    all_gather x1 -> x0, waiting for transfers between devices: 27.9 us -> none  [local(): all_columns = lax.all_gather(my_share, 'col', axis=1, tiled=True)]
    ppermute x0 -> x3, waiting for transfers between devices: none -> 23.3 us  [meet_fields(): lax.ppermute(samples[-1], axis_name=across, perm=[(no, (no + 1) % how_man...]
  transfers between devices with their start and end apart: 7 -> 9, of which waited for: 7 -> 9; matrix products, arithmetic and copies ran while one was open for 19% -> 19% of each run, Pallas kernels for 0% -> 0%
where the time goes in v1:
time: 389 us
  waiting for transfers between devices  232 us (60%)
  other arithmetic  91.3 us (23%)
  matrix products  26.7 us (7%)
  local copies, waits for them, and re-layouts  21.7 us (6%)
  between operations  14.6 us (4%)
    all_gather x1, waiting for transfers between devices, local(): factor_rows = lax.all_gather(local_factor, 'col', axis=0, tiled=True)  80.8 us
    another operation x6, other arithmetic, local(): jax.scipy.linalg.solve_triangular(diag_block, current[offset:offset + PAN...  79.9 us
    reduce_scatter x1, waiting for transfers between devices, local(): lax.psum_scatter(lax.dot_general(spread, my_columns, (((0,), (0,)), ((),...  69.9 us
    psum x4, waiting for transfers between devices, spread_2(): return lax.psum(kept, axis)  57.7 us
    ppermute x3, waiting for transfers between devices, meet_fields(): lax.ppermute(samples[-1], axis_name=across, perm=[(no, (no + 1) % how_man...  23.3 us
    another operation x29, local copies, waits for them, and re-layouts, local(): jax.scipy.linalg.solve_triangular(diag_block, current[offset:offset + PAN...  15.5 us
    dot_general x4, matrix products, local(): update = jnp.dot(panel_cols, solved, preferred_element_type=jnp.float32)  13.4 us
  transfers between devices with their start and end apart: 9, of which 9 were waited for; matrix products, arithmetic and copies ran while one was open for 19% of the time, Pallas kernels for 0%

profile of v1, /device:TPU:0, one launch (start us, length us, event | category | flops | bytes accessed | tf_op | source)
XLA Modules:
  0.0 388.9 jit_solution(10532520779711605961)
XLA Ops:
  8.8 3.5 convert_select_fusion
  12.3 80.8 %all-gather.3.cloned.1.call-done = bf16[1,2048,1024]{2,1,0:T(8,128)(2,1)} async-done(((bf16[1,512,1024]{2,1,0:T(8,128)(2,1)}), bf16[1,2048,1024]{2,1,0:T(8,128)(2,1)}) %all-gather.3.cloned.1.call-update) | async-done | bytes 4194320 | tf_op jit(solution)/shard_map/all_gather | solution.py:71
  94.3 3.8 while.12
  98.1 19.7 %custom-call.6 = f32[2,128,128]{1,2,0:T(8,128)S(1)} custom-call(f32[2,128,128]{2,1,0:T(8,128)S(1)} %get-tuple-element.77), custom_call_target="InvertDiagBlocksLowerTriangular" | custom-call | tf_op jit(solution)/shard_map/jit(_solve_triangular)/triangular_solve | solution.py:78
  121.7 4.0 %while.13 = (s32[]{:T(128)}, f32[256,256]{1,0:T(8,128)S(1)}, s32[2,2]{1,0:T(2,128)S(1)}, f32[2,128,128]{2,1,0:T(8,128)S(1)}, s32[]{:T(128)}) while((s32[]{:T(128)}, f32[256,256]{1,0:T(8,128)S(1)}, s32[2,2]{1,0:T(2,128)S(1)}, f32[2,128,128]{2,1,0:T(8,128)S(1)}, s32[]{:T(128)}) %tuple.111), condition=%wide.while_cond.4.clone, body=%wide.while_body.4.clone.sunk | while | flops 2 | bytes 131181 | solution.py:78
  125.8 19.7 %custom-call.7 = f32[2,128,128]{1,2,0:T(8,128)S(1)} custom-call(f32[2,128,128]{2,1,0:T(8,128)S(1)} %get-tuple-element.78), custom_call_target="InvertDiagBlocksLowerTriangular" | custom-call | tf_op jit(solution)/shard_map/jit(_solve_triangular)/triangular_solve | solution.py:78
  145.5 7.4 %all-reduce.5.cloned.1.call-done = bf16[256,512]{1,0:T(8,128)(2,1)} async-done(((bf16[256,512]{1,0:T(8,128)(2,1)}), bf16[256,512]{1,0:T(8,128)(2,1)}) %all-reduce.5.cloned.1.call-update) | async-done | bytes 262160 | tf_op jit(solution)/shard_map/psum | solution.py:35
  152.9 3.4 subtract_select_fusion.3
  160.2 4.0 %while.14 = (s32[]{:T(128)}, f32[256,256]{1,0:T(8,128)S(1)}, s32[2,2]{1,0:T(2,128)S(1)}, f32[2,128,128]{2,1,0:T(8,128)S(1)}, s32[]{:T(128)}) while((s32[]{:T(128)}, f32[256,256]{1,0:T(8,128)S(1)}, s32[2,2]{1,0:T(2,128)S(1)}, f32[2,128,128]{2,1,0:T(8,128)S(1)}, s32[]{:T(128)}) %tuple.112), condition=%wide.while_cond.4.clone.1, body=%wide.while_body.4.clone.1.sunk | while | flops 2 | bytes 131181 | solution.py:78
  164.2 19.7 %custom-call.8 = f32[2,128,128]{1,2,0:T(8,128)S(1)} custom-call(f32[2,128,128]{2,1,0:T(8,128)S(1)} %get-tuple-element.79), custom_call_target="InvertDiagBlocksLowerTriangular" | custom-call | tf_op jit(solution)/shard_map/jit(_solve_triangular)/triangular_solve | solution.py:78
  183.9 8.8 %all-reduce.7.cloned.1.call-done = bf16[256,512]{1,0:T(8,128)(2,1)} async-done(((bf16[256,512]{1,0:T(8,128)(2,1)}), bf16[256,512]{1,0:T(8,128)(2,1)}) %all-reduce.7.cloned.1.call-update) | async-done | bytes 262160 | tf_op jit(solution)/shard_map/psum | solution.py:35
  192.7 3.4 subtract_select_fusion.2
  199.9 3.8 while.15
  203.7 19.7 %custom-call.9 = f32[2,128,128]{1,2,0:T(8,128)S(1)} custom-call(f32[2,128,128]{2,1,0:T(8,128)S(1)} %get-tuple-element.80), custom_call_target="InvertDiagBlocksLowerTriangular" | custom-call | tf_op jit(solution)/shard_map/jit(_solve_triangular)/triangular_solve | solution.py:78
  223.4 9.2 %all-reduce.9.cloned.1.call-done = bf16[256,512]{1,0:T(8,128)(2,1)} async-done(((bf16[256,512]{1,0:T(8,128)(2,1)}), bf16[256,512]{1,0:T(8,128)(2,1)}) %all-reduce.9.cloned.1.call-update) | async-done | bytes 262160 | tf_op jit(solution)/shard_map/psum | solution.py:35
  232.5 3.4 subtract_select_fusion.1
  239.7 32.3 %all-reduce.11.cloned.1.call-done = bf16[256,512]{1,0:T(8,128)(2,1)} async-done(((bf16[256,512]{1,0:T(8,128)(2,1)}), bf16[256,512]{1,0:T(8,128)(2,1)}) %all-reduce.11.cloned.1.call-update) | async-done | bytes 262160 | tf_op jit(solution)/shard_map/psum | solution.py:35
  272.0 3.4 subtract_select_fusion
  277.8 7.0 %collective-permute-done = bf16[256,512]{1,0:T(8,128)(2,1)S(1)} collective-permute-done((bf16[256,512]{1,0:T(8,128)(2,1)S(1)}, bf16[256,512]{1,0:T(8,128)(2,1)S(1)}, u32[]{:S(2)}, u32[]{:S(2)}) %collective-permute-start) | collective-permute-done | bytes 262176 | tf_op jit(solution)/shard_map/ppermute | solution.py:18
  284.8 8.2 %collective-permute-done.1 = bf16[256,512]{1,0:T(8,128)(2,1)S(1)} collective-permute-done((bf16[256,512]{1,0:T(8,128)(2,1)S(1)}, bf16[256,512]{1,0:T(8,128)(2,1)S(1)}, u32[]{:S(2)}, u32[]{:S(2)}) %collective-permute-start.1) | collective-permute-done | bytes 262176 | tf_op jit(solution)/shard_map/ppermute | solution.py:18
  293.0 8.2 %collective-permute-done.2 = bf16[256,512]{1,0:T(8,128)(2,1)S(1)} collective-permute-done((bf16[256,512]{1,0:T(8,128)(2,1)S(1)}, bf16[256,512]{1,0:T(8,128)(2,1)S(1)}, u32[]{:S(2)}, u32[]{:S(2)}) %collective-permute-start.2) | collective-permute-done | bytes 262176 | tf_op jit(solution)/shard_map/ppermute | solution.py:18
  303.6 5.6 %convolution_convert_fusion = bf16[4096,1024]{1,0:T(8,128)(2,1)} fusion(bf16[256,4096]{1,0:T(8,128)(2,1)S(1)} %bitcast.105, s32[]{:T(128)S(6)} %select_n.141), kind=kOutput, calls=%fused_computation.8 | convolution fusion | flops 2151677952 | bytes 11010052 | tf_op jit(solution)/shard_map/dot_general | solution.py:96
  309.3 69.9 %reduce-scatter.2.cloned.1.call-done = bf16[512,1024]{1,0:T(8,128)(2,1)} async-done(((bf16[4096,1024]{1,0:T(8,128)(2,1)}), bf16[512,1024]{1,0:T(8,128)(2,1)}) %reduce-scatter.2.cloned.1.call-update) | async-done | bytes 1048592 | tf_op jit(solution)/shard_map/reduce_scatter | solution.py:95
  379.2 2.8 convert_subtract_fusion
  (107 shorter events, 38.3 us)
Async XLA Ops:
  7.2 85.9 %all-gather.3.cloned.1.call-start = ((), (), s32[]{:S(2)}) async-start(), calls=%async_computation.6 | async-start | bytes 5242880 | tf_op jit(solution)/shard_map/all_gather | solution.py:71
  7.9 145.0 %all-reduce.5.cloned.1.call-start = ((), (), s32[]{:S(2)}) async-start(), calls=%async_computation.1 | async-start | bytes 524288 | tf_op jit(solution)/shard_map/psum | solution.py:35
  12.3 140.6 %copy-start.6 = (bf16[1,2048,512]{2,1,0:T(8,128)(2,1)S(1)}, bf16[1,2048,512]{2,1,0:T(8,128)(2,1)}, u32[]{:S(2)}) copy-start(bf16[1,2048,512]{2,1,0:T(8,128)(2,1)} %param.16) | copy-start | bytes 6291460
  121.7 71.0 %all-reduce.7.cloned.1.call-start = ((), (), s32[]{:S(2)}) async-start(), calls=%async_computation.2 | async-start | bytes 524288 | tf_op jit(solution)/shard_map/psum | solution.py:35
  152.9 3.4 copy-start.8
  156.4 2.0 copy-start.2
  160.0 72.6 %all-reduce.9.cloned.1.call-start = ((), (), s32[]{:S(2)}) async-start(), calls=%async_computation.3 | async-start | bytes 524288 | tf_op jit(solution)/shard_map/psum | solution.py:35
  192.7 3.4 copy-start.4
  196.2 2.0 copy-start.1
  199.8 72.2 %all-reduce.11.cloned.1.call-start = ((), (), s32[]{:S(2)}) async-start(), calls=%async_computation.4 | async-start | bytes 524288 | tf_op jit(solution)/shard_map/psum | solution.py:35
  232.5 3.4 copy-start.5
  236.0 2.0 copy-start
  239.6 139.6 %reduce-scatter.2.cloned.1.call-start = ((), (), s32[]{:S(2)}) async-start(), calls=%async_computation.5 | async-start | bytes 9437184 | tf_op jit(solution)/shard_map/reduce_scatter | solution.py:95
  272.0 3.4 copy-start.9
  276.3 25.6 %copy-start.3 = (bf16[2048,512]{1,0:T(8,128)(2,1)}, bf16[2048,512]{1,0:T(8,128)(2,1)S(1)}, u32[]{:S(2)}) copy-start(bf16[2048,512]{1,0:T(8,128)(2,1)S(1)} %get-tuple-element.126) | copy-start | bytes 6291460
  276.3 8.5 %collective-permute-start = (bf16[256,512]{1,0:T(8,128)(2,1)S(1)}, bf16[256,512]{1,0:T(8,128)(2,1)S(1)}, u32[]{:S(2)}, u32[]{:S(2)}) collective-permute-start(bf16[256,512]{1,0:T(8,128)(2,1)S(1)} %get-tuple-element.125), channel_id=1, source_target_pairs={{0,1},{1,2},{2,3},{3,0},{4,5},{5,6},{6,7},{7,4},{8,9},{9,10},{10,1... | collective-permute-start | bytes 786440 | tf_op jit(solution)/shard_map/ppermute | solution.py:18
  284.8 8.2 %collective-permute-start.1 = (bf16[256,512]{1,0:T(8,128)(2,1)S(1)}, bf16[256,512]{1,0:T(8,128)(2,1)S(1)}, u32[]{:S(2)}, u32[]{:S(2)}) collective-permute-start(bf16[256,512]{1,0:T(8,128)(2,1)S(1)} %collective-permute-done), channel_id=1, source_target_pairs={{0,1},{1,2},{2,3},{3,0},{4,5},{5,6},{6,7},{7,4},{8,9},{9,10},{10,1... | collective-permute-start | bytes 786440 | tf_op jit(solution)/shard_map/ppermute | solution.py:18
  293.0 8.2 %collective-permute-start.2 = (bf16[256,512]{1,0:T(8,128)(2,1)S(1)}, bf16[256,512]{1,0:T(8,128)(2,1)S(1)}, u32[]{:S(2)}, u32[]{:S(2)}) collective-permute-start(bf16[256,512]{1,0:T(8,128)(2,1)S(1)} %collective-permute-done.1), channel_id=1, source_target_pairs={{0,1},{1,2},{2,3},{3,0},{4,5},{5,6},{6,7},{7,4},{8,9},{9,10},{10,1... | collective-permute-start | bytes 786440 | tf_op jit(solution)/shard_map/ppermute | solution.py:18
  293.0 8.9 %copy-start.10 = (s32[1,8]{1,0:T(1,128)S(1)}, s32[1,8]{1,0:T(1,128)}, u32[]{:S(2)}) copy-start(s32[1,8]{1,0:T(1,128)} %param.18) | copy-start | bytes 100
  309.2 70.0 %copy-start.7 = (f32[512,1024]{1,0:T(8,128)S(1)}, f32[512,1024]{1,0:T(8,128)}, u32[]{:S(2)}) copy-start(f32[512,1024]{1,0:T(8,128)} %param.19) | copy-start | bytes 6291460
Sparse Core Ops, SparseCore 0:
  9.5 83.4 all-gather.2
  121.8 31.0 all-reduce.4
  160.1 32.5 all-reduce.6
  199.9 32.5 all-reduce.8
  239.7 32.2 all-reduce.10
  309.4 69.7 reduce-scatter.1
